TPU v7x, 32 devices: a whole 2x2x4 slice. The times are simulated.
32 devices in a mesh: section: 4 (over y, core), sim: 8 (over z, x).
Axes of the slice: x: 2, y: 2, z: 4, core: 2. Of those that a mesh axis runs over, the one named last changes fastest.
Arguments:
- state: float32 [128, 64, 8192], P('section', None, 'sim'), may hold values from -60 to 60
- owner: int32 [128, 1], P('section'), may hold values from 0 to 7; in each aligned block of 32 rows (0 to 31, 32 to 63, ...) at most 8 rows name the same one
- counts: int32 [128], P('section'), may hold values from 2048 to 8192
Outputs:
- slab_mean: float32 [128, 64], P('section')
- slab_cov: float32 [128, 4096], P('section', 'sim')
- group_cov: float32 [32, 4096], P(('section', 'sim'))
- global_mean: float32 [64], replicated
- global_cov: float32 [64, 64], replicated
Inputs may be any that keep to these rules, and one draw needn't show every extreme that they name: Among the 32 slabs of one group, no owner is named by more than 8 slabs, and one owner is named by exactly 8 slabs in some or all groups.
All inputs are finite; a program needn't handle non-finite values.
Results may differ from a plain program's by a relative error of at most 0.0003.
Values sent between devices are 32-bit elements; how exact they have to be, the bound alone decides.
A program may use at most 64 MiB of HBM per device.

v0:
```python
import jax
import jax.numpy as jnp
from jax import lax
from jax.sharding import PartitionSpec as P


def slot_payload(number, mean, comoment, capacity, n_sim, width):
    slot_cov = comoment / jnp.maximum(number - 1.0, 1.0)[:, None]
    cov_parts = slot_cov.reshape(capacity, n_sim, width * width // n_sim)
    mean_copies = jnp.broadcast_to(mean[:, None, :], (capacity, n_sim, width))
    return (cov_parts, mean_copies)


def owner_stats(number, mean, comoment):
    high = lax.Precision.HIGHEST
    width = mean.shape[1]
    group_count = jnp.sum(number)
    group_mean = jnp.sum(number[:, None] * mean, axis=0) / jnp.maximum(group_count, 1.0)
    offset = mean - group_mean[None, :]
    group_co = jnp.sum(comoment, axis=0) + jnp.einsum(
        "k,kv,kw->vw", number, offset, offset, precision=high
    ).reshape(width * width)
    return (group_count, group_mean, group_co)


def local(state, owner, counts):
    high = lax.Precision.HIGHEST
    slab_here, width, cells_dev = state.shape
    n_sim = lax.axis_size("sim")
    my_index = lax.axis_index("sim")
    capacity = 2 * slab_here // n_sim
    slots = n_sim * capacity
    target = owner[:, 0]
    order = jnp.arange(slab_here, dtype=jnp.int32)
    earlier = (target[:, None] == target[None, :]) & (order[None, :] < order[:, None])
    rank = jnp.sum(earlier.astype(jnp.int32), axis=1)
    slot_of = target * capacity + rank
    match = slot_of[:, None] == jnp.arange(slots, dtype=jnp.int32)[None, :]
    filled = jnp.any(match, axis=0)
    source_slab = jnp.sum(jnp.where(match, order[:, None], 0), axis=0)
    tile_start = my_index * cells_dev
    tile_count = jnp.clip(counts - tile_start, 0, cells_dev).astype(jnp.float32)
    live = jnp.arange(cells_dev, dtype=jnp.int32)[None, :] + tile_start < counts[:, None]
    tile_mean = (
        jnp.sum(jnp.where(live[:, None, :], state, 0.0), axis=2)
        / jnp.maximum(tile_count, 1.0)[:, None]
    )
    centered = jnp.where(live[:, None, :], state - tile_mean[:, :, None], 0.0)
    tile_co = jnp.einsum("svc,swc->svw", centered, centered, precision=high).reshape(
        slab_here, width * width
    )
    send_mean = jnp.where(filled[:, None], tile_mean[source_slab], 0.0).reshape(
        n_sim, capacity, width
    )
    send_co = jnp.where(filled[:, None], tile_co[source_slab], 0.0).reshape(
        n_sim, capacity, width * width
    )
    send_count = jnp.where(filled, tile_count[source_slab], 0.0).reshape(n_sim, capacity)
    means = lax.all_to_all(send_mean, "sim", split_axis=0, concat_axis=0, tiled=True)
    comoms = lax.all_to_all(send_co, "sim", split_axis=0, concat_axis=0, tiled=True)
    amounts = lax.all_to_all(send_count, "sim", split_axis=0, concat_axis=0, tiled=True)
    number = jnp.sum(amounts, axis=0)
    mean = jnp.sum(amounts[:, :, None] * means, axis=0) / jnp.maximum(number, 1.0)[:, None]
    offset = means - mean[None, :, :]
    extra = jnp.einsum("ik,ikv,ikw->kvw", amounts, offset, offset, precision=high)
    number, mean, comoment = (
        number,
        mean,
        jnp.sum(comoms, axis=0) + extra.reshape(number.shape[0], width * width),
    )
    cov_parts, mean_copies = slot_payload(number, mean, comoment, capacity, n_sim, width)
    back_cov, back_mean = (
        lax.all_to_all(cov_parts, "sim", split_axis=1, concat_axis=0, tiled=True),
        lax.all_to_all(mean_copies, "sim", split_axis=1, concat_axis=0, tiled=True),
    )
    slab_cov = back_cov[slot_of, 0]
    slab_mean = back_mean[slot_of, 0]
    group_count, group_mean, group_co = owner_stats(number, mean, comoment)
    group_cov = (group_co / jnp.maximum(group_count - 1.0, 1.0))[None, :]
    total, weighted = lax.psum((group_count, group_count * group_mean), ("section", "sim"))
    global_mean = weighted / total
    gap = group_mean - global_mean
    spread = lax.psum(group_co + group_count * jnp.outer(gap, gap).reshape(-1), ("section", "sim"))
    global_cov = (spread / (total - 1.0)).reshape(width, width)
    return (slab_mean, slab_cov, group_cov, global_mean, global_cov)


def solution(mesh):
    return jax.shard_map(
        local,
        mesh=mesh,
        in_specs=(P("section", None, "sim"), P("section", None), P("section")),
        out_specs=(P("section", None), P("section", "sim"), P(("section", "sim"), None), P(), P()),
        check_vma=False,
    )
```

profile of v0, /device:TPU:0, one launch (start us, length us, event | category | flops | bytes accessed | tf_op | source)
XLA Modules:
  0.0 160.8 jit_solution(15916009984353185825)
XLA Ops:
  0.6 0.9 convert_reduce_fusion
  1.5 0.7 fusion.19
  2.2 0.1 fusion.10
  2.3 0.1 select_reduce_fusion.1
  2.4 0.7 broadcast_maximum_fusion.1
  3.1 0.8 gather_fusion
  3.9 0.7 select_n.56
  4.5 7.3 %all-to-all-start = ((f32[8,1,8]{2,1,0:T(1,128)}), f32[8,1,8]{2,1,0:T(1,128)S(1)}, u32[]{:S(2)}, u32[]{:S(2)}) async-start(f32[8,1,8]{2,1,0:T(1,128)} %bitcast.5), calls=%async_computation | async-start | bytes 8192 | tf_op jit(solution)/shard_map/all_to_all | solution.py:61
  11.8 0.1 broadcast_in_dim.63
  11.9 0.7 broadcast_compare_fusion
  12.7 4.1 %select_reduce_fusion = f32[32,64]{1,0:T(8,128)S(1)} fusion(f32[32,64,1024]{2,1,0:T(8,128)} %param.3, pred[32,1024]{1,0:T(8,128)(4,1)S(1)} %broadcast_compare_fusion), kind=kLoop, calls=%fused_computation.8 | loop fusion | flops 4192256 | bytes 8429568 | tf_op jit(solution)/shard_map/reduce_sum | solution.py:45
  16.8 0.1 broadcast_divide_fusion.2
  16.9 0.6 gather_fusion.1
  17.5 14.9 %fusion = f32[32,64,64]{2,1,0:T(8,128)S(1)} fusion(f32[32,64,1024]{2,1,0:T(8,128)} %param.3, f32[32,64]{1,0:T(8,128)S(1)} %broadcast_divide_fusion.2, pred[32,1024]{1,0:T(8,128)(4,1)S(1)} %broadcast_compare_fusion), kind=kOutput, calls=%fused_computation.5 | convolution fusion | flops 1614807040 | bytes 8953856 | tf_op jit(solution)/shard_map/svc,swc->svw/dot_general | solution.py:49
  32.4 0.1 bitcast_select_fusion.1
  32.5 0.7 reshape.244
  33.2 0.4 reshape.205
  33.5 0.9 gather_fusion.3
  34.5 0.0 all-to-all-done
  34.5 6.0 %all-to-all-start.1 = ((f32[8,1,512]{2,1,0:T(1,128)}), f32[8,1,512]{2,1,0:T(1,128)S(1)}, u32[]{:S(2)}, u32[]{:S(2)}) async-start(f32[8,1,512]{2,1,0:T(1,128)} %reshape.244), calls=%async_computation.1 | async-start | bytes 32768 | tf_op jit(solution)/shard_map/all_to_all | solution.py:59
  40.5 0.6 fusion.22
  41.1 6.0 %all-to-all-done.1 = f32[8,1,512]{2,1,0:T(1,128)S(1)} async-done(((f32[8,1,512]{2,1,0:T(1,128)}), f32[8,1,512]{2,1,0:T(1,128)S(1)}, u32[]{:S(2)}, u32[]{:S(2)}) %all-to-all-start.1) | async-done | bytes 16416 | tf_op jit(solution)/shard_map/all_to_all | solution.py:59
  47.1 0.5 broadcast.202
  47.6 0.7 reduce.4
  48.3 0.1 reshape.245
  48.3 0.1 multiply_reduce_fusion
  48.4 0.1 multiply_reduce_fusion.1
  48.5 0.7 reshape.246
  49.2 3.3 %all-to-all-start.2 = ((f32[8,1,512]{2,1,0:T(1,128)}), f32[8,1,512]{2,1,0:T(1,128)S(1)}, u32[]{:S(2)}, u32[]{:S(2)}) async-start(f32[8,1,512]{2,1,0:T(1,128)} %reshape.246), calls=%async_computation.2 | async-start | bytes 32768 | tf_op jit(solution)/shard_map/all_to_all | solution.py:74
  52.6 1.1 bitcast_select_fusion
  53.7 5.4 %all-to-all-done.2 = f32[8,1,512]{2,1,0:T(1,128)S(1)} async-done(((f32[8,1,512]{2,1,0:T(1,128)}), f32[8,1,512]{2,1,0:T(1,128)S(1)}, u32[]{:S(2)}, u32[]{:S(2)}) %all-to-all-start.2) | async-done | bytes 16416 | tf_op jit(solution)/shard_map/all_to_all | solution.py:74
  59.1 3.6 %all-to-all-start.3 = ((f32[8,8,4096]{2,1,0:T(8,128)}), f32[8,8,4096]{2,1,0:T(8,128)S(1)}, u32[]{:S(2)}, u32[]{:S(2)}) async-start(f32[8,8,4096]{2,1,0:T(8,128)} %bitcast_select_fusion), calls=%async_computation.3 | async-start | bytes 2097152 | tf_op jit(solution)/shard_map/all_to_all | solution.py:60
  63.9 0.7 broadcast_multiply_fusion.1
  64.6 41.6 %all-reduce.1 = (f32[64]{0:T(128)S(1)}, f32[]{:T(128)}) all-reduce(f32[64]{0:T(128)S(1)} %get-tuple-element.11, f32[]{:T(128)} %get-tuple-element.5), channel_id=1, replica_groups=mesh['section'=4,'sim'=8] {'section','sim'}, use_global_device_ids=true, to_apply=%region_10.11 | all-reduce | flops 65 | bytes 520 | tf_op jit(solution)/shard_map/psum | solution.py:80
  106.8 1.2 fusion.23
  108.0 0.1 broadcast_multiply_fusion
  108.1 0.7 reduce.5
  108.8 0.1 reshape.247
  108.8 1.2 gather_fusion.2
  110.0 0.0 all-to-all-done.3
  110.0 0.1 reduce_sum.96
  110.1 0.1 reduce_sum.98
  110.2 0.6 add_reduce_fusion
  110.8 0.1 reshape.206
  110.9 0.7 fusion.6
  111.7 5.3 %all-to-all-start.4 = ((f32[8,8,512]{2,0,1:T(8,128)}), f32[8,8,512]{2,0,1:T(8,128)S(1)}, u32[]{:S(2)}, u32[]{:S(2)}) async-start(f32[8,8,512]{2,0,1:T(8,128)} %fusion.6), calls=%async_computation.4 | async-start | bytes 262144 | tf_op jit(solution)/shard_map/all_to_all | solution.py:73
  117.0 1.0 multiply_add_fusion
  117.9 0.7 div.85
  118.6 0.1 add.82
  118.7 40.0 %psum.23 = f32[4096]{0:T(1024)S(1)} all-reduce(f32[4096]{0:T(1024)S(1)} %add.82), channel_id=1, replica_groups=mesh['section'=4,'sim'=8] {'section','sim'}, use_global_device_ids=true, to_apply=%region_12.13 | all-reduce | flops 4096 | bytes 32768 | tf_op jit(solution)/shard_map/psum | solution.py:83
  158.7 0.7 reshape.207
  159.4 0.0 all-to-all-done.4
  159.4 0.1 all_to_all.46
  159.6 1.2 gather_fusion.4
  (7 shorter events, 0.0 us)
Async XLA Ops:
  4.5 29.9 %all-to-all-start = ((f32[8,1,8]{2,1,0:T(1,128)}), f32[8,1,8]{2,1,0:T(1,128)S(1)}, u32[]{:S(2)}, u32[]{:S(2)}) async-start(f32[8,1,8]{2,1,0:T(1,128)} %bitcast.5), calls=%async_computation | async-start | bytes 8192 | tf_op jit(solution)/shard_map/all_to_all | solution.py:61
  34.5 12.6 %all-to-all-start.1 = ((f32[8,1,512]{2,1,0:T(1,128)}), f32[8,1,512]{2,1,0:T(1,128)S(1)}, u32[]{:S(2)}, u32[]{:S(2)}) async-start(f32[8,1,512]{2,1,0:T(1,128)} %reshape.244), calls=%async_computation.1 | async-start | bytes 32768 | tf_op jit(solution)/shard_map/all_to_all | solution.py:59
  49.2 9.9 %all-to-all-start.2 = ((f32[8,1,512]{2,1,0:T(1,128)}), f32[8,1,512]{2,1,0:T(1,128)S(1)}, u32[]{:S(2)}, u32[]{:S(2)}) async-start(f32[8,1,512]{2,1,0:T(1,128)} %reshape.246), calls=%async_computation.2 | async-start | bytes 32768 | tf_op jit(solution)/shard_map/all_to_all | solution.py:74
  59.1 51.0 %all-to-all-start.3 = ((f32[8,8,4096]{2,1,0:T(8,128)}), f32[8,8,4096]{2,1,0:T(8,128)S(1)}, u32[]{:S(2)}, u32[]{:S(2)}) async-start(f32[8,8,4096]{2,1,0:T(8,128)} %bitcast_select_fusion), calls=%async_computation.3 | async-start | bytes 2097152 | tf_op jit(solution)/shard_map/all_to_all | solution.py:60
  111.7 47.8 %all-to-all-start.4 = ((f32[8,8,512]{2,0,1:T(8,128)}), f32[8,8,512]{2,0,1:T(8,128)S(1)}, u32[]{:S(2)}, u32[]{:S(2)}) async-start(f32[8,8,512]{2,0,1:T(8,128)} %fusion.6), calls=%async_computation.4 | async-start | bytes 262144 | tf_op jit(solution)/shard_map/all_to_all | solution.py:73
where the time goes:
time: 162 us; the launch traced here: 161 us
  blocking collectives  81.6 us (50%)
  starting transfers between devices  25.5 us (16%)
  matrix products  16.5 us (10%)
  other arithmetic  13.4 us (8%)
  waiting for transfers between devices  11.3 us (7%)
  local copies, waits for them, and re-layouts  9.73 us (6%)
  between operations  2.71 us (2%)
    psum x1, blocking collectives, local(): lax.psum((group_count, group_count * group_mean), ('section', 'sim'))  41.6 us
    psum x1, blocking collectives, local(): lax.psum(group_co + group_count * jnp.outer(gap, gap).reshape(-1), ('sect...  40 us
    dot_general x1, matrix products, local(): jnp.einsum('svc,swc->svw', centered, centered, precision=high)  14.9 us
    all_to_all x1, starting transfers between devices, local(): lax.all_to_all(send_count, 'sim', split_axis=0, concat_axis=0, tiled=True)  7.28 us
    all_to_all x1, starting transfers between devices, local(): lax.all_to_all(send_mean, 'sim', split_axis=0, concat_axis=0, tiled=True)  6.01 us
    all_to_all x1, waiting for transfers between devices, local(): lax.all_to_all(send_mean, 'sim', split_axis=0, concat_axis=0, tiled=True)  5.96 us
    all_to_all x1, waiting for transfers between devices, local(): lax.all_to_all(mean_copies, 'sim', split_axis=1, concat_axis=0, tiled=True)  5.37 us
    all_to_all x1, starting transfers between devices, local(): lax.all_to_all(cov_parts, 'sim', split_axis=1, concat_axis=0, tiled=True)  5.31 us
  transfers between devices with their start and end apart: 5, of which 2 were waited for; matrix products, arithmetic and copies ran while one was open for 19% of the time, Pallas kernels for 0%

commit v1 on v0

--- a/solution.py
+++ b/solution.py
@@ -80,7 +80,9 @@
     total, weighted = lax.psum((group_count, group_count * group_mean), ("section", "sim"))
     global_mean = weighted / total
     gap = group_mean - global_mean
-    spread = lax.psum(group_co + group_count * jnp.outer(gap, gap).reshape(-1), ("section", "sim"))
+    own = group_co + group_count * jnp.outer(gap, gap).reshape(-1)
+    parts = lax.all_gather(own, ("section", "sim"))
+    spread = jnp.sum(parts, axis=0)
     global_cov = (spread / (total - 1.0)).reshape(width, width)
     return (slab_mean, slab_cov, group_cov, global_mean, global_cov)
 

time: 162 us -> 191 us (1.18)
  blocking collectives: 81.6 us -> 111 us
    all_gather x0 -> x1, blocking collectives: none -> 69.1 us  [local(): parts = lax.all_gather(own, ('section', 'sim'))]
    psum x1 -> x0, blocking collectives: 40 us -> none  [local(): lax.psum(group_co + group_count * jnp.outer(gap, gap).reshape(-1), ('sect...]
  transfers between devices with their start and end apart: 5 -> 5, of which waited for: 2 -> 2; matrix products, arithmetic and copies ran while one was open for 19% -> 16% of each run, Pallas kernels for 0% -> 0%
where the time goes in v1:
time: 191 us; the launch traced here: 190 us
  blocking collectives  111 us (58%)
  starting transfers between devices  25.5 us (13%)
  matrix products  16.5 us (9%)
  other arithmetic  13.8 us (7%)
  waiting for transfers between devices  11.3 us (6%)
  local copies, waits for them, and re-layouts  9.74 us (5%)
  between operations  2.72 us (1%)
    all_gather x1, blocking collectives, local(): parts = lax.all_gather(own, ('section', 'sim'))  69.1 us
    psum x1, blocking collectives, local(): lax.psum((group_count, group_count * group_mean), ('section', 'sim'))  41.6 us
    dot_general x1, matrix products, local(): jnp.einsum('svc,swc->svw', centered, centered, precision=high)  14.9 us
    all_to_all x1, starting transfers between devices, local(): lax.all_to_all(send_count, 'sim', split_axis=0, concat_axis=0, tiled=True)  7.28 us
    all_to_all x1, starting transfers between devices, local(): lax.all_to_all(send_mean, 'sim', split_axis=0, concat_axis=0, tiled=True)  6.01 us
    all_to_all x1, waiting for transfers between devices, local(): lax.all_to_all(send_mean, 'sim', split_axis=0, concat_axis=0, tiled=True)  5.96 us
    all_to_all x1, waiting for transfers between devices, local(): lax.all_to_all(mean_copies, 'sim', split_axis=1, concat_axis=0, tiled=True)  5.37 us
    all_to_all x1, starting transfers between devices, local(): lax.all_to_all(cov_parts, 'sim', split_axis=1, concat_axis=0, tiled=True)  5.31 us
  transfers between devices with their start and end apart: 5, of which 2 were waited for; matrix products, arithmetic and copies ran while one was open for 16% of the time, Pallas kernels for 0%

profile of v1, /device:TPU:0, one launch (start us, length us, event | category | flops | bytes accessed | tf_op | source)
XLA Modules:
  0.0 190.2 jit_solution(1760976473713318403)
XLA Ops:
  0.6 0.9 convert_reduce_fusion
  1.5 0.7 fusion.19
  2.2 0.1 fusion.10
  2.3 0.1 select_reduce_fusion.1
  2.4 0.7 broadcast_maximum_fusion.1
  3.1 0.8 gather_fusion
  3.9 0.7 select_n.56
  4.5 7.3 %all-to-all-start = ((f32[8,1,8]{2,1,0:T(1,128)}), f32[8,1,8]{2,1,0:T(1,128)S(1)}, u32[]{:S(2)}, u32[]{:S(2)}) async-start(f32[8,1,8]{2,1,0:T(1,128)} %bitcast.5), calls=%async_computation | async-start | bytes 8192 | tf_op jit(solution)/shard_map/all_to_all | solution.py:61
  11.8 0.1 broadcast_in_dim.63
  11.9 0.7 broadcast_compare_fusion
  12.7 4.1 %select_reduce_fusion = f32[32,64]{1,0:T(8,128)S(1)} fusion(f32[32,64,1024]{2,1,0:T(8,128)} %param.3, pred[32,1024]{1,0:T(8,128)(4,1)S(1)} %broadcast_compare_fusion), kind=kLoop, calls=%fused_computation.8 | loop fusion | flops 4192256 | bytes 8429568 | tf_op jit(solution)/shard_map/reduce_sum | solution.py:45
  16.8 0.1 broadcast_divide_fusion.2
  16.9 0.6 gather_fusion.1
  17.5 14.9 %fusion = f32[32,64,64]{2,1,0:T(8,128)S(1)} fusion(f32[32,64,1024]{2,1,0:T(8,128)} %param.3, f32[32,64]{1,0:T(8,128)S(1)} %broadcast_divide_fusion.2, pred[32,1024]{1,0:T(8,128)(4,1)S(1)} %broadcast_compare_fusion), kind=kOutput, calls=%fused_computation.5 | convolution fusion | flops 1614807040 | bytes 8953856 | tf_op jit(solution)/shard_map/svc,swc->svw/dot_general | solution.py:49
  32.4 0.1 bitcast_select_fusion.1
  32.5 0.7 reshape.278
  33.2 0.4 reshape.237
  33.5 0.9 gather_fusion.3
  34.5 0.0 all-to-all-done
  34.5 6.0 %all-to-all-start.1 = ((f32[8,1,512]{2,1,0:T(1,128)}), f32[8,1,512]{2,1,0:T(1,128)S(1)}, u32[]{:S(2)}, u32[]{:S(2)}) async-start(f32[8,1,512]{2,1,0:T(1,128)} %reshape.278), calls=%async_computation.1 | async-start | bytes 32768 | tf_op jit(solution)/shard_map/all_to_all | solution.py:59
  40.5 0.6 fusion.22
  41.1 6.0 %all-to-all-done.1 = f32[8,1,512]{2,1,0:T(1,128)S(1)} async-done(((f32[8,1,512]{2,1,0:T(1,128)}), f32[8,1,512]{2,1,0:T(1,128)S(1)}, u32[]{:S(2)}, u32[]{:S(2)}) %all-to-all-start.1) | async-done | bytes 16416 | tf_op jit(solution)/shard_map/all_to_all | solution.py:59
  47.1 0.5 broadcast.212
  47.6 0.7 reduce.5
  48.3 0.1 reshape.279
  48.3 0.1 multiply_reduce_fusion
  48.4 0.1 multiply_reduce_fusion.1
  48.5 0.7 reshape.280
  49.2 3.3 %all-to-all-start.2 = ((f32[8,1,512]{2,1,0:T(1,128)}), f32[8,1,512]{2,1,0:T(1,128)S(1)}, u32[]{:S(2)}, u32[]{:S(2)}) async-start(f32[8,1,512]{2,1,0:T(1,128)} %reshape.280), calls=%async_computation.2 | async-start | bytes 32768 | tf_op jit(solution)/shard_map/all_to_all | solution.py:74
  52.6 1.1 bitcast_select_fusion
  53.7 5.4 %all-to-all-done.2 = f32[8,1,512]{2,1,0:T(1,128)S(1)} async-done(((f32[8,1,512]{2,1,0:T(1,128)}), f32[8,1,512]{2,1,0:T(1,128)S(1)}, u32[]{:S(2)}, u32[]{:S(2)}) %all-to-all-start.2) | async-done | bytes 16416 | tf_op jit(solution)/shard_map/all_to_all | solution.py:74
  59.1 3.6 %all-to-all-start.3 = ((f32[8,8,4096]{2,1,0:T(8,128)}), f32[8,8,4096]{2,1,0:T(8,128)S(1)}, u32[]{:S(2)}, u32[]{:S(2)}) async-start(f32[8,8,4096]{2,1,0:T(8,128)} %bitcast_select_fusion), calls=%async_computation.3 | async-start | bytes 2097152 | tf_op jit(solution)/shard_map/all_to_all | solution.py:60
  63.9 0.7 broadcast_multiply_fusion.1
  64.6 41.6 %all-reduce.1 = (f32[64]{0:T(128)S(1)}, f32[]{:T(128)}) all-reduce(f32[64]{0:T(128)S(1)} %get-tuple-element.11, f32[]{:T(128)} %get-tuple-element.5), channel_id=1, replica_groups=mesh['section'=4,'sim'=8] {'section','sim'}, use_global_device_ids=true, to_apply=%region_10.11 | all-reduce | flops 65 | bytes 520 | tf_op jit(solution)/shard_map/psum | solution.py:80
  106.8 1.2 fusion.23
  108.0 0.1 broadcast_multiply_fusion
  108.1 0.7 reduce.6
  108.8 0.1 reshape.281
  108.8 1.2 gather_fusion.2
  110.0 0.0 all-to-all-done.3
  110.0 0.1 reduce_sum.105
  110.1 0.1 reduce_sum.107
  110.2 0.6 add_reduce_fusion
  110.8 0.1 reshape.238
  110.9 0.7 fusion.6
  111.7 5.3 %all-to-all-start.4 = ((f32[8,8,512]{2,0,1:T(8,128)}), f32[8,8,512]{2,0,1:T(8,128)S(1)}, u32[]{:S(2)}, u32[]{:S(2)}) async-start(f32[8,8,512]{2,0,1:T(8,128)} %fusion.6), calls=%async_computation.4 | async-start | bytes 262144 | tf_op jit(solution)/shard_map/all_to_all | solution.py:73
  117.0 1.0 multiply_add_fusion
  117.9 0.1 reshape.275
  118.0 69.1 %all-gather = f32[32,1,4096]{2,1,0:T(1,128)S(1)} all-gather(f32[1,1,4096]{2,1,0:T(1,128)S(1)} %reshape.275), channel_id=1, replica_groups=mesh['section'=4,'sim'=8] {'section','sim'}, dimensions={0}, use_global_device_ids=true | all-gather | bytes 540672 | tf_op jit(solution)/shard_map/all_gather | solution.py:84
  187.1 0.7 div.89
  187.8 0.4 reduce_sum.111
  188.2 0.7 div.94
  188.8 0.0 all-to-all-done.4
  188.9 0.1 all_to_all.46
  189.0 1.2 gather_fusion.4
  (7 shorter events, 0.0 us)
Async XLA Ops:
  4.5 29.9 %all-to-all-start = ((f32[8,1,8]{2,1,0:T(1,128)}), f32[8,1,8]{2,1,0:T(1,128)S(1)}, u32[]{:S(2)}, u32[]{:S(2)}) async-start(f32[8,1,8]{2,1,0:T(1,128)} %bitcast.5), calls=%async_computation | async-start | bytes 8192 | tf_op jit(solution)/shard_map/all_to_all | solution.py:61
  34.5 12.6 %all-to-all-start.1 = ((f32[8,1,512]{2,1,0:T(1,128)}), f32[8,1,512]{2,1,0:T(1,128)S(1)}, u32[]{:S(2)}, u32[]{:S(2)}) async-start(f32[8,1,512]{2,1,0:T(1,128)} %reshape.278), calls=%async_computation.1 | async-start | bytes 32768 | tf_op jit(solution)/shard_map/all_to_all | solution.py:59
  49.2 9.9 %all-to-all-start.2 = ((f32[8,1,512]{2,1,0:T(1,128)}), f32[8,1,512]{2,1,0:T(1,128)S(1)}, u32[]{:S(2)}, u32[]{:S(2)}) async-start(f32[8,1,512]{2,1,0:T(1,128)} %reshape.280), calls=%async_computation.2 | async-start | bytes 32768 | tf_op jit(solution)/shard_map/all_to_all | solution.py:74
  59.1 51.0 %all-to-all-start.3 = ((f32[8,8,4096]{2,1,0:T(8,128)}), f32[8,8,4096]{2,1,0:T(8,128)S(1)}, u32[]{:S(2)}, u32[]{:S(2)}) async-start(f32[8,8,4096]{2,1,0:T(8,128)} %bitcast_select_fusion), calls=%async_computation.3 | async-start | bytes 2097152 | tf_op jit(solution)/shard_map/all_to_all | solution.py:60
  111.7 77.2 %all-to-all-start.4 = ((f32[8,8,512]{2,0,1:T(8,128)}), f32[8,8,512]{2,0,1:T(8,128)S(1)}, u32[]{:S(2)}, u32[]{:S(2)}) async-start(f32[8,8,512]{2,0,1:T(8,128)} %fusion.6), calls=%async_computation.4 | async-start | bytes 262144 | tf_op jit(solution)/shard_map/all_to_all | solution.py:73
